TPU v7x, 256 devices: a whole 4x4x8 slice. The times are simulated.
256 devices in a mesh: mem: 32 (over x_lo, z, core), space: 8 (over x_hi, y).
Axes of the slice: x: 4 (x_hi: 2, x_lo: 2; x = x_hi * 2 + x_lo), y: 4, z: 8, core: 2. Of those that a mesh axis runs over, the one named last changes fastest.
Arguments:
- prior_samples: bfloat16 [256, 128, 8192], P('mem', 'space'), may hold values from -6 to 6
- diffusivity_field: float32 [128, 8192], P('space'), may hold values from 0.05 to 0.24
- measured_site_position: int32 [8, 32, 512], P('space', 'mem'), may hold values from 0 to 4095
- measured_quantities: float32 [8, 32, 512], P('space', 'mem'), may hold values from -6 to 6
- measurement_weightings: float32 [8, 32, 512], P('space', 'mem'), may hold values from 0.5 to 8
Outputs:
- analysis: bfloat16 [256, 128, 8192], P('mem', 'space')
Inputs may be any that keep to these rules, and one draw needn't show every extreme that they name: measured_site_position[p, q, o] names cell a * 256 + b of patch (p, q) itself.
All inputs are finite; a program needn't handle non-finite values.
Results may differ from a plain program's by a relative error of at most 0.0077.
Values may be sent and summed in bfloat16 or wider, within the bound.
No kernel may reach another device: no remote copies, remote signals or barrier semaphores. Data moves between devices by JAX's collectives and lax.ppermute only.
A program may use at most 64 MiB of HBM per device.

v0:
```python
import jax
import jax.numpy as jnp
from jax import lax
from jax.experimental import pallas as pl
from jax.experimental.pallas import tpu as pltpu
from jax.sharding import Mesh
from jax.sharding import PartitionSpec as P

ITERS = 10
MEM = ("mem_0", "mem_1", "mem_2")
F32 = jnp.float32
BF16 = jnp.bfloat16
VMEM_LIMIT = 24 << 20


def params():
    return pltpu.CompilerParams(vmem_limit_bytes=VMEM_LIMIT)


def is_odd():
    return lax.bitwise_and(lax.axis_index("space"), 1) > 0


def vmem_specs(count):
    return [pl.BlockSpec(memory_space=pltpu.VMEM) for _ in range(count)]


def sides(window):
    width = window.shape[1]
    both = pltpu.roll(window, 1, axis=1) + pltpu.roll(window, width - 1, axis=1)
    return both[:, 128 : width - 128]


def sweep(load, coef_ref, put, first, count, shift, off, width):
    above = load(first - 1)[:, 128 : 128 + width]
    here = load(first)
    for r in range(first, first + count):
        below = load(r + 1)
        mid = here[:, 128 : 128 + width]
        lap = (above + below[:, 128 : 128 + width]) + sides(here) - 4.0 * mid
        put(r, mid + coef_ref[r + shift : r + shift + 1, pl.ds(off, width)] * lap)
        above, here = mid, below


def edges_of(index, width, total):
    off = pl.multiple_of(index * width, width)
    before = pl.multiple_of(jnp.maximum(off - 128, 0), 128)
    after = pl.multiple_of(jnp.minimum(off + width, total - 128), 128)
    return off, before, after


def framed(left, mid, right, index, count):
    left = jnp.where(index > 0, left, 0.0)
    right = jnp.where(index < count - 1, right, 0.0)
    return jnp.concatenate([left, mid, right], axis=1)


CHUNK = 512


def ends_kernel(x_hbm, field_hbm, one_ref, two_ref, x_ref, field_ref, arrived):
    members, rows, width = x_ref.shape
    odd = is_odd()
    parts = arrived.shape[0] - 1
    size = width // parts

    def fetch(k):
        where = slice(k * size, (k + 1) * size)
        return pltpu.make_async_copy(x_hbm.at[:, :, where], x_ref.at[:, :, where], arrived.at[k])

    whole = pltpu.make_async_copy(field_hbm, field_ref, arrived.at[parts])
    whole.start()
    for k in range(parts):
        fetch(k).start()

    def put(where, low, high):
        one_ref[:, where] = jnp.where(odd, low, high).astype(BF16)
        two_ref[:, where] = jnp.where(odd, high, low).astype(BF16)

    piece = width // members

    def folded(row):
        lines = [field_ref[row : row + 1, s * piece : (s + 1) * piece] for s in range(members)]
        block = jnp.concatenate(lines, axis=0)
        return [part.astype(F32) for part in halves(block)]

    whole.wait()
    for k, (low, high) in enumerate(zip(folded(0), folded(rows - 1))):
        begin = 2 * width + k * piece
        put(slice(begin, begin + piece), low, high)

    def some(c, carry):
        off = pl.multiple_of(c * CHUNK, CHUNK)
        tall = [x_ref[m, :, pl.ds(off, CHUNK)].astype(F32) for m in range(members)]
        for k in range(2):
            low = jnp.concatenate([t[k : k + 1] for t in tall], axis=0)
            high = jnp.concatenate([t[rows - 2 + k : rows - 1 + k] for t in tall], axis=0)
            put(pl.ds(pl.multiple_of(k * width + off, CHUNK), CHUNK), low, high)
        return carry

    each = size // CHUNK
    for k in range(parts):
        fetch(k).wait()
        lax.fori_loop(k * each, (k + 1) * each, some, 0, unroll=2)


def ends(x, field):
    members, _, width = x.shape
    shape = jax.ShapeDtypeStruct((members, 2 * width + 2 * width // members), BF16)
    return pl.pallas_call(
        ends_kernel,
        out_shape=(
            shape,
            shape,
            jax.ShapeDtypeStruct(x.shape, x.dtype),
            jax.ShapeDtypeStruct(field.shape, field.dtype),
        ),
        in_specs=[pl.BlockSpec(memory_space=pltpu.HBM)] * 2,
        out_specs=tuple(vmem_specs(4)),
        scratch_shapes=[pltpu.SemaphoreType.DMA((5,))],
        compiler_params=params(),
        name="ends",
    )(*(pltpu.with_memory_space_constraint(v, pltpu.HBM) for v in (x, field)))


def first_pass(source, coef_ref, keep, index, width, spans, shift):
    off, before, after = edges_of(index, CHUNK, width)

    def load(r):
        pieces = [source(r, o, s) for o, s in ((before, 128), (off, CHUNK), (after, 128))]
        return framed(*pieces, index, width // CHUNK)

    for begin, count in spans:

        def put(r, value):
            keep(r, pl.ds(off, CHUNK), value)

        sweep(load, coef_ref, put, begin, count, shift, off, CHUNK)


def second_pass(coef_ref, pick, out_ref, index, width, spans, shift):
    cols = width // out_ref.shape[0]
    each = CHUNK // cols
    off, before, after = edges_of(index, CHUNK, width)

    def load(r):
        pieces = [pick(r, o, s) for o, s in ((before, 128), (off, CHUNK), (after, 128))]
        return framed(*pieces, index, width // CHUNK)

    def put(r, value):
        for k in range(each):
            out_ref[index * each + k, :, r * cols : (r + 1) * cols] = value[
                :, k * cols : (k + 1) * cols
            ].astype(BF16)

    for begin, count in spans:
        sweep(load, coef_ref, put, begin, count, shift, off, CHUNK)


def inner_kernel(x_ref, field_ref, out_ref, kept_ref, v1_ref):
    rows, _, width = x_ref.shape
    chunks = width // CHUNK
    kept = (1, 2, rows - 3, rows - 2)

    def first(c, carry):
        def source(r, off, size):
            return x_ref[r, :, pl.ds(off, size)].astype(F32)

        def keep(r, where, value):
            v1_ref[r + 1, :, where] = value
            if r in kept:
                kept_ref[kept.index(r), :, where] = value

        first_pass(source, field_ref, keep, c, width, ((1, rows - 2),), 0)
        return carry

    def pick(r, off, size):
        return v1_ref[r + 1, :, pl.ds(off, size)]

    def second(c, carry):
        second_pass(field_ref, pick, out_ref, c, width, ((2, rows - 4),), 0)
        return carry

    lax.fori_loop(0, chunks, first, 0, unroll=4)
    lax.fori_loop(0, chunks, second, 0, unroll=4)


def inner_forecast(x, field, patches):
    rows, members, width = x.shape
    return pl.pallas_call(
        inner_kernel,
        out_shape=(
            jax.ShapeDtypeStruct((patches, members, rows * width // patches), BF16),
            jax.ShapeDtypeStruct((4, members, width), F32),
        ),
        in_specs=vmem_specs(2),
        out_specs=tuple(vmem_specs(2)),
        scratch_shapes=[pltpu.VMEM((rows + 2, members, width), F32)],
        compiler_params=params(),
        name="inner",
    )(x, field)


def outer_kernel(x_ref, one_ref, two_ref, field_ref, part_ref, kept_ref, out_ref, v1_ref, coef_ref):
    rows, members, width = x_ref.shape
    del part_ref
    odd = is_odd()
    piece = width // members
    coef_ref[pl.ds(8, rows), :] = field_ref[...]
    one = one_ref[:, 2 * width :].astype(F32)
    two = two_ref[:, 2 * width :].astype(F32)
    one = one[:, :piece] + one[:, piece:]
    two = two[:, :piece] + two[:, piece:]
    low = jnp.where(odd, one, two)
    high = jnp.where(odd, two, one)
    for s in range(members):
        coef_ref[7:8, s * piece : (s + 1) * piece] = low[s : s + 1]
        coef_ref[8 + rows : 9 + rows, s * piece : (s + 1) * piece] = high[s : s + 1]

    def first(c, carry):
        def source(r, off, size):
            if 0 <= r < rows:
                return x_ref[r, :, pl.ds(off, size)].astype(F32)
            at = (r + 2 if r < 0 else r - rows) * width
            a = one_ref[:, pl.ds(at + off, size)].astype(F32)
            b = two_ref[:, pl.ds(at + off, size)].astype(F32)
            return jnp.where(odd, a, b) if r < 0 else jnp.where(odd, b, a)

        def keep(r, where, value):
            v1_ref[r + 1, :, where] = value

        first_pass(source, coef_ref, keep, c, width, ((-1, 2), (rows - 1, 2)), 8)
        return carry

    kept = (1, 2, rows - 3, rows - 2)

    def pick(r, off, size):
        if r in kept:
            return kept_ref[kept.index(r), :, pl.ds(off, size)]
        return v1_ref[r + 1, :, pl.ds(off, size)]

    def second(c, carry):
        second_pass(coef_ref, pick, out_ref, c, width, ((0, 2), (rows - 2, 2)), 8)
        return carry

    lax.fori_loop(0, width // CHUNK, first, 0, unroll=4)
    lax.fori_loop(0, width // CHUNK, second, 0, unroll=4)


def outer_forecast(x, one, two, field, part, kept):
    rows, members, width = x.shape
    return pl.pallas_call(
        outer_kernel,
        out_shape=jax.ShapeDtypeStruct(part.shape, BF16),
        in_specs=vmem_specs(6),
        out_specs=pl.BlockSpec(memory_space=pltpu.VMEM),
        scratch_shapes=[pltpu.VMEM((rows + 2, members, width), F32), pltpu.VMEM((rows + 16, width), F32)],
        input_output_aliases={4: 0},
        compiler_params=params(),
        name="outer",
    )(x, one, two, field, part, kept)


def gram_kernel(block_ref, site_ref, value_ref, weight_ref, out_ref):
    groups, each, cells = block_ref.shape
    members = groups * each
    count = site_ref.shape[1]
    half = members // 2
    step = 512
    site = site_ref[...]
    observed = jnp.zeros((members, count), F32)
    for c in range(cells // step):
        cell = lax.broadcasted_iota(jnp.int32, (step, count), 0) + c * step
        chosen = jnp.where(cell == site, 1.0, 0.0).astype(BF16)
        piece = block_ref[:, :, c * step : (c + 1) * step].reshape(members, step)
        observed += jnp.dot(piece, chosen, preferred_element_type=F32)
    mean = jnp.sum(observed, axis=0, keepdims=True) * (1.0 / members)
    root = jnp.sqrt(weight_ref[...])
    spread = ((observed - mean) * root).astype(BF16)
    innovation = ((value_ref[...] - mean) * root).astype(BF16)
    tail = jnp.broadcast_to(innovation.astype(F32), (16, count)).astype(BF16)
    left = jnp.concatenate([spread, tail], axis=0)
    both = lax.dot_general(left, spread, (((1,), (1,)), ((), ())), preferred_element_type=F32)
    low = both[half:members, half:]
    across = lax.broadcasted_iota(jnp.int32, (half, half), 0)
    along = lax.broadcasted_iota(jnp.int32, (half, half), 1)
    corner = jnp.sum(jnp.where(across == along, low, 0.0), axis=0, keepdims=True)
    out_ref[:half, :half] = jnp.where(across <= along, both[:half, :half], low)
    out_ref[:half, half:] = both[:half, half:]
    out_ref[half:, :] = both[members : members + 8]
    out_ref[half + 1 : half + 2, :half] = corner


def gram_of(blocks, sites, values, weights):
    members = blocks.shape[0] * blocks.shape[1]
    return pl.pallas_call(
        gram_kernel,
        out_shape=jax.ShapeDtypeStruct((members // 2 + 8, members), F32),
        in_specs=vmem_specs(4),
        out_specs=pl.BlockSpec(memory_space=pltpu.VMEM),
        compiler_params=params(),
        name="gram",
    )(blocks, sites, values, weights)


def unpacked(packed, half):
    across = lax.broadcasted_iota(jnp.int32, (half, half), 0)
    along = lax.broadcasted_iota(jnp.int32, (half, half), 1)
    block = packed[:half, :half]
    turned = block.T
    upper = jnp.where(across <= along, block, turned)
    lower = jnp.where(across > along, block, turned)
    lower = jnp.where(across == along, packed[half + 1 : half + 2, :half], lower)
    side = packed[:half, half:]
    return jnp.concatenate(
        [jnp.concatenate([upper, side], axis=1), jnp.concatenate([side.T, lower], axis=1)], axis=0
    )


def halves(value):
    high = value.astype(BF16)
    return high, (value - high.astype(F32)).astype(BF16)


def product(left, right):
    lh, ll = left
    rh, rl = right
    return (
        jnp.dot(lh, rh, preferred_element_type=F32)
        + jnp.dot(lh, rl, preferred_element_type=F32)
        + jnp.dot(ll, rh, preferred_element_type=F32)
    )


def root_kernel(one_ref, mid_ref, two_ref, out_ref, root_ref, inverse_ref):
    members = out_ref.shape[0]
    half = members // 2
    packed = mid_ref[...] + 0.5 * (one_ref[...] + two_ref[...])
    vector = packed[half : half + 8]
    gram = unpacked(packed, half)
    across = lax.broadcasted_iota(jnp.int32, (members, members), 0)
    along = lax.broadcasted_iota(jnp.int32, (members, members), 1)
    on_diagonal = across == along
    system = jnp.where(on_diagonal, gram + (members - 1.0), gram)
    squares = jnp.sum(jnp.sum(system * system, axis=0, keepdims=True), axis=1, keepdims=True)
    frob = jnp.sqrt(squares)
    root = system / frob

    def factor_of(value):
        return jnp.where(on_diagonal, 1.5 - 0.5 * value, -0.5 * value)

    def keep(ref, pair):
        ref[0], ref[1] = pair

    def kept(ref):
        return ref[0], ref[1]

    factor_h = halves(factor_of(root))
    keep(inverse_ref, factor_h)
    keep(root_ref, halves(product(halves(root), factor_h)))

    def newton(step, carry):
        factor_h = halves(factor_of(product(kept(inverse_ref), kept(root_ref))))
        new_root = product(kept(root_ref), factor_h)
        new_inverse = product(factor_h, kept(inverse_ref))
        keep(root_ref, halves(new_root))
        keep(inverse_ref, halves(new_inverse))
        return carry

    lax.fori_loop(1, ITERS - 1, newton, 0)
    factor_h = halves(factor_of(product(kept(inverse_ref), kept(root_ref))))
    inverse = product(factor_h, kept(inverse_ref))
    inverse_h = halves(inverse)
    weights = product(halves(product(halves(vector), inverse_h)), inverse_h) / frob
    scale = jnp.sqrt(members - 1.0) * lax.rsqrt(frob)
    out_ref[...] = (scale * inverse + weights[0:1]).astype(BF16)


def root_of(one, mid, two):
    members = mid.shape[1]
    return pl.pallas_call(
        root_kernel,
        out_shape=jax.ShapeDtypeStruct((members, members), BF16),
        in_specs=vmem_specs(3),
        out_specs=pl.BlockSpec(memory_space=pltpu.VMEM),
        scratch_shapes=[pltpu.VMEM((2, members, members), BF16)] * 2,
        compiler_params=params(),
        name="root",
    )(one, mid, two)


def center_kernel(block_ref, mean_ref, out_ref):
    groups, each, cells = block_ref.shape
    members = groups * each
    step = 256

    def one(c, carry):
        where = pl.ds(pl.multiple_of(c * step, step), step)
        cellwise = block_ref[:, :, where].astype(F32)
        mean = jnp.sum(jnp.sum(cellwise, axis=0), axis=0, keepdims=True) * (1.0 / members)
        mean_ref[:, where] = mean
        out_ref[:, where] = (cellwise.reshape(members, step) - mean).astype(BF16)
        return carry

    lax.fori_loop(0, cells // step, one, 0, unroll=2)


def centered(blocks):
    groups, each, cells = blocks.shape
    return pl.pallas_call(
        center_kernel,
        out_shape=(
            jax.ShapeDtypeStruct((1, cells), F32),
            jax.ShapeDtypeStruct((groups * each, cells), BF16),
        ),
        in_specs=vmem_specs(1),
        out_specs=tuple(vmem_specs(2)),
        compiler_params=params(),
        name="center",
    )(blocks)


def update_kernel(turned_ref, mean_ref, deviation_ref, out_ref):
    groups, each, cells = out_ref.shape
    step = 512

    def one(c, carry):
        where = pl.ds(pl.multiple_of(c * step, step), step)
        moved = jnp.dot(turned_ref[...], deviation_ref[:, where], preferred_element_type=F32)
        out_ref[:, :, where] = (mean_ref[:, where] + moved).reshape(groups, each, step).astype(BF16)
        return carry

    lax.fori_loop(0, cells // step, one, 0, unroll=2)


def update(turned, mean, deviation, shape):
    return pl.pallas_call(
        update_kernel,
        out_shape=jax.ShapeDtypeStruct(shape, BF16),
        in_specs=vmem_specs(3),
        out_specs=pl.BlockSpec(memory_space=pltpu.VMEM),
        compiler_params=params(),
        name="update",
    )(turned, mean, deviation)


def edges_kernel(block_ref, one_ref, two_ref):
    cols = one_ref.shape[2]
    odd = is_odd()
    for q in range(block_ref.shape[0]):
        first = block_ref[q, :, :cols].astype(F32)
        last = block_ref[q, :, -cols:].astype(F32)
        one_ref[q] = jnp.where(odd, first, last).astype(BF16)
        two_ref[q] = jnp.where(odd, last, first).astype(BF16)


def edges(blocks, cols):
    shape = jax.ShapeDtypeStruct((*blocks.shape[:2], cols), BF16)
    return pl.pallas_call(
        edges_kernel,
        out_shape=(shape, shape),
        in_specs=vmem_specs(1),
        out_specs=tuple(vmem_specs(2)),
        compiler_params=params(),
        name="edges",
    )(blocks)


def final_rows(source, coef_ref, put, index, cols, patches, spans):
    each = CHUNK // cols
    base = index * each
    off = pl.multiple_of(index * CHUNK, CHUNK)
    before = jnp.maximum(base - 1, 0)
    after = jnp.minimum(base + each, patches - 1)

    def load(r):
        left = source(r, before, cols - 128, cols)
        mid = jnp.concatenate([source(r, base + k, 0, cols) for k in range(each)], axis=1)
        return framed(left, mid, source(r, after, 0, 128), index, patches // each)

    for begin, count in spans:
        sweep(load, coef_ref, put, begin, count, 0, off, CHUNK)


def middle_kernel(block_ref, coef_ref, out_ref, ends_ref, lines_ref):
    patches, members, cells = block_ref.shape
    rows = coef_ref.shape[0]
    cols = cells // rows
    pitch = rows + 8
    lines_ref[...] = jnp.zeros_like(lines_ref)

    def one(c, carry):
        off = pl.multiple_of(c * CHUNK, CHUNK)

        def source(r, q, begin, end):
            if not 0 <= r < rows:
                return jnp.zeros((members, end - begin), F32)
            return block_ref[q, :, r * cols + begin : r * cols + end].astype(F32)

        def put(r, value):
            if r in (0, rows - 1):
                ends_ref[min(r, 1), :, pl.ds(off, CHUNK)] = value
                return
            for k in range(CHUNK // 128):
                lines_ref[k, pl.ds(r, members, stride=pitch), :] = value[:, k * 128 : (k + 1) * 128]

        final_rows(source, coef_ref, put, c, cols, patches, ((0, rows),))
        for m in range(members):
            tiles = [lines_ref[k, m * pitch : m * pitch + rows, :] for k in range(CHUNK // 128)]
            out_ref[m, :, pl.ds(off, CHUNK)] = jnp.concatenate(tiles, axis=1).astype(BF16)
        return carry

    lax.fori_loop(0, patches * cols // CHUNK, one, 0, unroll=2)


def middle_rows(blocks, coef):
    _, members, _ = blocks.shape
    rows, width = coef.shape
    return pl.pallas_call(
        middle_kernel,
        out_shape=(
            jax.ShapeDtypeStruct((members, rows, width), BF16),
            jax.ShapeDtypeStruct((2, members, width), F32),
        ),
        in_specs=vmem_specs(2),
        out_specs=tuple(vmem_specs(2)),
        scratch_shapes=[pltpu.VMEM((CHUNK // 128, members * (rows + 8), 128), F32)],
        compiler_params=params(),
        name="middle",
    )(blocks, coef)


def rim_kernel(one_ref, two_ref, coef_ref, part_ref, start_ref, out_ref, whole_ref, ends_ref, done):
    members, rows, width = part_ref.shape
    cols = one_ref.shape[2]
    each = CHUNK // cols
    chunks = width // CHUNK
    odd = is_odd()
    line = lax.broadcasted_iota(jnp.int32, (rows, CHUNK), 0)

    def move(c):
        where = pl.ds(pl.multiple_of(c * CHUNK, CHUNK), CHUNK)
        return pltpu.make_async_copy(whole_ref.at[:, :, where], out_ref.at[:, :, where], done.at[c])

    def one(c, carry):
        where = pl.ds(pl.multiple_of(c * CHUNK, CHUNK), CHUNK)
        a = jnp.concatenate([one_ref[c * each + k].astype(F32) for k in range(each)], axis=1)
        b = jnp.concatenate([two_ref[c * each + k].astype(F32) for k in range(each)], axis=1)
        for k, beside in enumerate((jnp.where(odd, a, b), jnp.where(odd, b, a))):
            r = k * (rows - 1)
            ends_ref[k, :, where] = start_ref[k, :, where] + coef_ref[r : r + 1, where] * beside
        for m in range(members):
            old = part_ref[m, :, where].astype(F32)
            new = jnp.where(line == 0, ends_ref[0, m : m + 1, where], old)
            new = jnp.where(line == rows - 1, ends_ref[1, m : m + 1, where], new)
            whole_ref[m, :, where] = new.astype(BF16)
        move(c).start()
        return carry

    lax.fori_loop(0, chunks, one, 0, unroll=4)

    def settle(c, carry):
        move(c).wait()
        return carry

    lax.fori_loop(0, chunks, settle, 0)


def rim_rows(one, two, coef, part, start):
    members, _, width = part.shape
    return pl.pallas_call(
        rim_kernel,
        out_shape=jax.ShapeDtypeStruct(part.shape, BF16),
        in_specs=vmem_specs(5),
        out_specs=pl.BlockSpec(memory_space=pl.ANY),
        scratch_shapes=[
            pltpu.VMEM(part.shape, BF16),
            pltpu.VMEM((2, members, width), F32),
            pltpu.SemaphoreType.DMA((width // CHUNK,)),
        ],
        compiler_params=params(),
        name="rim",
    )(one, two, coef, part, start)


def swaps(axis, in_one, in_two):
    count = lax.axis_size(axis)

    def pairs(first):
        both = [(i, i + 1) for i in range(first, count - 1, 2)]
        return both + [(j, i) for i, j in both]

    two = lax.ppermute(in_two, axis, pairs(1))
    one = lax.ppermute(in_one, axis, pairs(0))
    return one, two


def body(
    prior_samples,
    diffusivity_field,
    measured_site_position,
    measured_quantities,
    measurement_weightings,
):
    patches = lax.axis_size(MEM)
    cols = prior_samples.shape[2] // patches
    one, two, prior, field = ends(prior_samples, diffusivity_field)
    one, two = swaps("space", one, two)
    turned_prior = jnp.swapaxes(prior, 0, 1)
    part, kept = inner_forecast(turned_prior, field, patches)
    blocks = outer_forecast(turned_prior, one, two, field, part, kept)
    gathered = lax.all_to_all(blocks, MEM, 0, 0, tiled=True)
    own = gram_of(
        gathered, measured_site_position[0], measured_quantities[0], measurement_weightings[0]
    )
    one, two = swaps(MEM, own, own)
    mean, deviation = centered(gathered)
    band = own + 0.5 * (one + two)
    one, two = swaps("space", band, band)
    updated = update(root_of(one, band, two), mean, deviation, gathered.shape)
    returned = lax.all_to_all(updated, MEM, 0, 0, tiled=True)
    one, two = swaps("space", *edges(returned, cols))
    part, start = middle_rows(returned, field)
    return rim_rows(one, two, field, part, start)


def solution(mesh):
    finer = Mesh(
        mesh.devices.reshape(2, 8, 2, mesh.shape["space"]), ("mem_0", "mem_1", "mem_2", "space")
    )
    in_specs = (
        P(MEM, "space", None),
        P("space", None),
        P("space", MEM, None),
        P("space", MEM, None),
        P("space", MEM, None),
    )
    out_specs = P(MEM, "space", None)
    return jax.shard_map(body, mesh=finer, in_specs=in_specs, out_specs=out_specs, check_vma=False)
```

profile of v0, /device:TPU:56, one launch (start us, length us, event | category | flops | bytes accessed | tf_op | source)
XLA Modules:
  0.0 173.8 jit_solution(7455446443142567869)
XLA Ops:
  0.0 2.0 %ends.1 = (bf16[8,18432]{1,0:T(8,128)(2,1)S(1)}, bf16[8,18432]{1,0:T(8,128)(2,1)S(1)}, bf16[8,16,8192]{2,1,0:T(8,128)(2,1)S(1)}, f32[16,8192]{1,0:T(8,128)S(1)}) custom-call(bf16[8,16,8192]{2,1,0:T(8,128)(2,1)} %x_hbm.1, f32[16,8192]{1,0:T(8,128)} %field_hbm.1), custom_call_target="tpu_custom_call" | custom-call | tf_op jit(solution)/shard_map/ends/pallas_call | solution.py:110
  2.0 0.8 collective-permute-start
  2.9 5.4 %collective-permute-start.1 = (bf16[8,18432]{1,0:T(8,128)(2,1)S(1)}, bf16[8,18432]{1,0:T(8,128)(2,1)S(1)}, u32[]{:S(2)}, u32[]{:S(2)}) collective-permute-start(bf16[8,18432]{1,0:T(8,128)(2,1)S(1)} %get-tuple-element.19), channel_id=1, source_target_pairs={{1,2},{3,4},{5,6},{2,1},{4,3},{6,5},{9,10},{11,12},{13,14},{10,9},... | collective-permute-start | bytes 884744 | tf_op jit(solution)/shard_map/ppermute | solution.py:593
  8.3 1.2 copy.9
  9.4 4.3 %inner.1 = (bf16[32,8,4096]{2,1,0:T(8,128)(2,1)S(1)}, f32[4,8,8192]{2,1,0:T(8,128)S(1)}) custom-call(bf16[16,8,8192]{2,1,0:T(8,128)(2,1)S(1)} %bitcast.6, f32[16,8192]{1,0:T(8,128)S(1)} %get-tuple-element.20.field_ref.coef_ref), custom_call_target="tpu_custom_call" | custom-call | tf_op jit(solution)/shard_map/inner/pallas_call | solution.py:190
  13.7 3.1 %collective-permute-done.1.two_ref = bf16[8,18432]{1,0:T(8,128)(2,1)S(1)} collective-permute-done((bf16[8,18432]{1,0:T(8,128)(2,1)S(1)}, bf16[8,18432]{1,0:T(8,128)(2,1)S(1)}, u32[]{:S(2)}, u32[]{:S(2)}) %collective-permute-start.1) | collective-permute-done | bytes 294944 | tf_op jit(solution)/shard_map/ppermute | solution.py:593
  16.8 1.7 %outer.1 = bf16[32,8,4096]{2,1,0:T(8,128)(2,1)S(1)} custom-call(bf16[16,8,8192]{2,1,0:T(8,128)(2,1)S(1)} %bitcast.7, bf16[8,18432]{1,0:T(8,128)(2,1)S(1)} %collective-permute-done.one_ref, bf16[8,18432]{1,0:T(8,128)(2,1)S(1)} %collective-permute-done.1.two_ref, f32[16,8192]{1,0:T(8,128)S(1)} %get-tuple-element.20.field_ref.coef_ref, ...), custom_call_target="tpu_custom_call", output_to_operand_aliasing={{}: (4, {})} | custom-call | tf_op jit(solution)/shard_map/outer/pallas_call | solution.py:252
  18.6 61.0 %all_to_all.10.block_ref = bf16[32,8,4096]{2,1,0:T(8,128)(2,1)S(1)} all-to-all(bf16[32,8,4096]{2,1,0:T(8,128)(2,1)S(1)} %outer.1), channel_id=1, replica_groups=mesh['mem_0'=2,'mem_1'=8,'mem_2'=2,'space'=8] {'mem_0','mem_1','mem_2'}, dimensions={0} | all-to-all | bytes 4194304 | tf_op jit(solution)/shard_map/all_to_all | solution.py:612
  79.6 1.6 gram.1
  81.2 1.9 %collective-permute-start.3 = (f32[136,256]{1,0:T(8,128)S(1)}, f32[136,256]{1,0:T(8,128)S(1)}, u32[]{:S(2)}, u32[]{:S(2)}) collective-permute-start(f32[136,256]{1,0:T(8,128)S(1)} %gram.1), channel_id=1, source_target_pairs={{8,16},{24,32},{40,48},{56,64},{72,80},{88,96},{104,112},{120,128}... | collective-permute-start | bytes 417800 | tf_op jit(solution)/shard_map/ppermute | solution.py:593
  83.2 0.1 collective-permute-start.2
  83.3 4.3 %collective-permute-done.3 = f32[136,256]{1,0:T(8,128)S(1)} collective-permute-done((f32[136,256]{1,0:T(8,128)S(1)}, f32[136,256]{1,0:T(8,128)S(1)}, u32[]{:S(2)}, u32[]{:S(2)}) %collective-permute-start.3) | collective-permute-done | bytes 139296 | tf_op jit(solution)/shard_map/ppermute | solution.py:593
  87.6 5.1 %collective-permute-start.5 = (f32[136,256]{1,0:T(8,128)S(1)}, f32[136,256]{1,0:T(8,128)S(1)}, u32[]{:S(2)}, u32[]{:S(2)}) collective-permute-start(f32[136,256]{1,0:T(8,128)S(1)} %multiply_add_fusion.mid_ref), channel_id=1, source_target_pairs={{1,2},{3,4},{5,6},{2,1},{4,3},{6,5},{9,10},{11,12},{13,14},{10,9},... | collective-permute-start | bytes 417800 | tf_op jit(solution)/shard_map/ppermute | solution.py:593
  92.8 0.1 collective-permute-start.4
  92.9 0.8 center.1
  93.7 4.5 %collective-permute-done.5.two_ref = f32[136,256]{1,0:T(8,128)S(1)} collective-permute-done((f32[136,256]{1,0:T(8,128)S(1)}, f32[136,256]{1,0:T(8,128)S(1)}, u32[]{:S(2)}, u32[]{:S(2)}) %collective-permute-start.5) | collective-permute-done | bytes 139296 | tf_op jit(solution)/shard_map/ppermute | solution.py:593
  98.2 6.4 %root.1.turned_ref = bf16[256,256]{1,0:T(8,128)(2,1)S(1)} custom-call(f32[136,256]{1,0:T(8,128)S(1)} %collective-permute-done.4.one_ref, f32[136,256]{1,0:T(8,128)S(1)} %multiply_add_fusion.mid_ref, f32[136,256]{1,0:T(8,128)S(1)} %collective-permute-done.5.two_ref), custom_call_target="tpu_custom_call" | custom-call | tf_op jit(solution)/shard_map/root/pallas_call | solution.py:381
  104.6 1.2 update.1
  105.9 55.8 %all_to_all.11.block_ref = bf16[32,8,4096]{2,1,0:T(8,128)(2,1)S(1)} all-to-all(bf16[32,8,4096]{2,1,0:T(8,128)(2,1)S(1)} %update.1), channel_id=1, replica_groups=mesh['mem_0'=2,'mem_1'=8,'mem_2'=2,'space'=8] {'mem_0','mem_1','mem_2'}, dimensions={0} | all-to-all | bytes 4194304 | tf_op jit(solution)/shard_map/all_to_all | solution.py:621
  161.7 0.1 collective-permute-start.6
  161.8 5.1 %collective-permute-start.7 = (bf16[32,8,256]{2,1,0:T(8,128)(2,1)S(1)}, bf16[32,8,256]{2,1,0:T(8,128)(2,1)S(1)}, u32[]{:S(2)}, u32[]{:S(2)}) collective-permute-start(bf16[32,8,256]{2,1,0:T(8,128)(2,1)S(1)} %get-tuple-element.26), channel_id=1, source_target_pairs={{1,2},{3,4},{5,6},{2,1},{4,3},{6,5},{9,10},{11,12},{13,14},{10,9},... | collective-permute-start | bytes 393224 | tf_op jit(solution)/shard_map/ppermute | solution.py:593
  167.0 2.6 %middle.1 = (bf16[8,16,8192]{2,1,0:T(8,128)(2,1)S(1)}, f32[2,8,8192]{2,1,0:T(8,128)S(1)}) custom-call(bf16[32,8,4096]{2,1,0:T(8,128)(2,1)S(1)} %all_to_all.11.block_ref, f32[16,8192]{1,0:T(8,128)S(1)} %get-tuple-element.20.field_ref.coef_ref), custom_call_target="tpu_custom_call" | custom-call | tf_op jit(solution)/shard_map/middle/pallas_call | solution.py:519
  169.5 2.8 %collective-permute-done.7.two_ref = bf16[32,8,256]{2,1,0:T(8,128)(2,1)S(1)} collective-permute-done((bf16[32,8,256]{2,1,0:T(8,128)(2,1)S(1)}, bf16[32,8,256]{2,1,0:T(8,128)(2,1)S(1)}, u32[]{:S(2)}, u32[]{:S(2)}) %collective-permute-start.7) | collective-permute-done | bytes 131104 | tf_op jit(solution)/shard_map/ppermute | solution.py:593
  172.3 1.5 rim.1
  (12 shorter events, 0.1 us)
Async XLA Ops:
  2.0 11.7 %collective-permute-start = (bf16[8,18432]{1,0:T(8,128)(2,1)S(1)}, bf16[8,18432]{1,0:T(8,128)(2,1)S(1)}, u32[]{:S(2)}, u32[]{:S(2)}) collective-permute-start(bf16[8,18432]{1,0:T(8,128)(2,1)S(1)} %get-tuple-element.18), channel_id=1, source_target_pairs={{0,1},{2,3},{4,5},{6,7},{1,0},{3,2},{5,4},{7,6},{8,9},{10,11},{12,... | collective-permute-start | bytes 884744 | tf_op jit(solution)/shard_map/ppermute | solution.py:594
  2.9 14.0 %collective-permute-start.1 = (bf16[8,18432]{1,0:T(8,128)(2,1)S(1)}, bf16[8,18432]{1,0:T(8,128)(2,1)S(1)}, u32[]{:S(2)}, u32[]{:S(2)}) collective-permute-start(bf16[8,18432]{1,0:T(8,128)(2,1)S(1)} %get-tuple-element.19), channel_id=1, source_target_pairs={{1,2},{3,4},{5,6},{2,1},{4,3},{6,5},{9,10},{11,12},{13,14},{10,9},... | collective-permute-start | bytes 884744 | tf_op jit(solution)/shard_map/ppermute | solution.py:593
  18.6 61.1 %copy-start = (s32[1,1,512]{2,1,0:T(1,128)S(1)}, s32[1,1,512]{2,1,0:T(1,128)}, u32[]{:S(2)}) copy-start(s32[1,1,512]{2,1,0:T(1,128)} %param.7) | copy-start | bytes 6148
  18.6 61.1 %copy-start.1 = (f32[1,1,512]{2,1,0:T(1,128)S(1)}, f32[1,1,512]{2,1,0:T(1,128)}, u32[]{:S(2)}) copy-start(f32[1,1,512]{2,1,0:T(1,128)} %param.8) | copy-start | bytes 6148
  18.6 61.0 %copy-start.2 = (f32[1,1,512]{2,1,0:T(1,128)S(1)}, f32[1,1,512]{2,1,0:T(1,128)}, u32[]{:S(2)}) copy-start(f32[1,1,512]{2,1,0:T(1,128)} %param.9) | copy-start | bytes 6148
  81.2 6.4 %collective-permute-start.3 = (f32[136,256]{1,0:T(8,128)S(1)}, f32[136,256]{1,0:T(8,128)S(1)}, u32[]{:S(2)}, u32[]{:S(2)}) collective-permute-start(f32[136,256]{1,0:T(8,128)S(1)} %gram.1), channel_id=1, source_target_pairs={{8,16},{24,32},{40,48},{56,64},{72,80},{88,96},{104,112},{120,128}... | collective-permute-start | bytes 417800 | tf_op jit(solution)/shard_map/ppermute | solution.py:593
  83.2 4.4 %collective-permute-start.2 = (f32[136,256]{1,0:T(8,128)S(1)}, f32[136,256]{1,0:T(8,128)S(1)}, u32[]{:S(2)}, u32[]{:S(2)}) collective-permute-start(f32[136,256]{1,0:T(8,128)S(1)} %gram.1), channel_id=1, source_target_pairs={{0,8},{16,24},{32,40},{48,56},{64,72},{80,88},{96,104},{112,120},{... | collective-permute-start | bytes 417800 | tf_op jit(solution)/shard_map/ppermute | solution.py:594
  87.6 10.6 %collective-permute-start.5 = (f32[136,256]{1,0:T(8,128)S(1)}, f32[136,256]{1,0:T(8,128)S(1)}, u32[]{:S(2)}, u32[]{:S(2)}) collective-permute-start(f32[136,256]{1,0:T(8,128)S(1)} %multiply_add_fusion.mid_ref), channel_id=1, source_target_pairs={{1,2},{3,4},{5,6},{2,1},{4,3},{6,5},{9,10},{11,12},{13,14},{10,9},... | collective-permute-start | bytes 417800 | tf_op jit(solution)/shard_map/ppermute | solution.py:593
  92.8 5.4 %collective-permute-start.4 = (f32[136,256]{1,0:T(8,128)S(1)}, f32[136,256]{1,0:T(8,128)S(1)}, u32[]{:S(2)}, u32[]{:S(2)}) collective-permute-start(f32[136,256]{1,0:T(8,128)S(1)} %multiply_add_fusion.mid_ref), channel_id=1, source_target_pairs={{0,1},{2,3},{4,5},{6,7},{1,0},{3,2},{5,4},{7,6},{8,9},{10,11},{12,... | collective-permute-start | bytes 417800 | tf_op jit(solution)/shard_map/ppermute | solution.py:594
  161.7 7.8 %collective-permute-start.6 = (bf16[32,8,256]{2,1,0:T(8,128)(2,1)S(1)}, bf16[32,8,256]{2,1,0:T(8,128)(2,1)S(1)}, u32[]{:S(2)}, u32[]{:S(2)}) collective-permute-start(bf16[32,8,256]{2,1,0:T(8,128)(2,1)S(1)} %get-tuple-element.25), channel_id=1, source_target_pairs={{0,1},{2,3},{4,5},{6,7},{1,0},{3,2},{5,4},{7,6},{8,9},{10,11},{12,... | collective-permute-start | bytes 393224 | tf_op jit(solution)/shard_map/ppermute | solution.py:594
  161.8 10.5 %collective-permute-start.7 = (bf16[32,8,256]{2,1,0:T(8,128)(2,1)S(1)}, bf16[32,8,256]{2,1,0:T(8,128)(2,1)S(1)}, u32[]{:S(2)}, u32[]{:S(2)}) collective-permute-start(bf16[32,8,256]{2,1,0:T(8,128)(2,1)S(1)} %get-tuple-element.26), channel_id=1, source_target_pairs={{1,2},{3,4},{5,6},{2,1},{4,3},{6,5},{9,10},{11,12},{13,14},{10,9},... | collective-permute-start | bytes 393224 | tf_op jit(solution)/shard_map/ppermute | solution.py:593
where the time goes:
time: 175 us; the launch traced here: 174 us
  blocking collectives  117 us (67%)
  Pallas kernels  22.1 us (13%)
  starting transfers between devices  18.7 us (11%)
  waiting for transfers between devices  14.7 us (8%)
    all_to_all x1, blocking collectives, body(): gathered = lax.all_to_all(blocks, MEM, 0, 0, tiled=True)  61 us
    all_to_all x1, blocking collectives, body(): returned = lax.all_to_all(updated, MEM, 0, 0, tiled=True)  55.8 us
    ppermute x4, starting transfers between devices, swaps(): two = lax.ppermute(in_two, axis, pairs(1))  17.6 us
    ppermute x4, waiting for transfers between devices, swaps(): two = lax.ppermute(in_two, axis, pairs(1))  14.7 us
    pallas_call x1, Pallas kernels, root_of(): pl.pallas_call(root_kernel, out_shape=jax.ShapeDtypeStruct((members, memb...  6.41 us
    pallas_call x1, Pallas kernels, inner_forecast(): pl.pallas_call(inner_kernel, out_shape=(jax.ShapeDtypeStruct((patches, me...  4.26 us
  transfers between devices with their start and end apart: 8, of which 4 were waited for; matrix products, arithmetic and copies ran while one was open for 1% of the time, Pallas kernels for 4%

commit v1 on v0

--- a/solution.py
+++ b/solution.py
@@ -117,7 +117,7 @@
         ),
         in_specs=[pl.BlockSpec(memory_space=pltpu.HBM)] * 2,
         out_specs=tuple(vmem_specs(4)),
-        scratch_shapes=[pltpu.SemaphoreType.DMA((5,))],
+        scratch_shapes=[pltpu.SemaphoreType.DMA((9,))],
         compiler_params=params(),
         name="ends",
     )(*(pltpu.with_memory_space_constraint(v, pltpu.HBM) for v in (x, field)))
@@ -325,10 +325,10 @@
 def product(left, right):
     lh, ll = left
     rh, rl = right
-    return (
-        jnp.dot(lh, rh, preferred_element_type=F32)
-        + jnp.dot(lh, rl, preferred_element_type=F32)
-        + jnp.dot(ll, rh, preferred_element_type=F32)
+    return jnp.dot(
+        jnp.concatenate([lh, lh, ll], axis=1),
+        jnp.concatenate([rh, rl, rh], axis=0),
+        preferred_element_type=F32,
     )
 
 

time: 175 us -> 175 us (level)
  no operation moved by 1% of the time
where the time goes in v1:
time: 175 us; the launch traced here: 174 us
  blocking collectives  117 us (67%)
  Pallas kernels  22.1 us (13%)
  starting transfers between devices  18.7 us (11%)
  waiting for transfers between devices  14.8 us (8%)
    all_to_all x1, blocking collectives, body(): gathered = lax.all_to_all(blocks, MEM, 0, 0, tiled=True)  61 us
    all_to_all x1, blocking collectives, body(): returned = lax.all_to_all(updated, MEM, 0, 0, tiled=True)  55.8 us
    ppermute x4, starting transfers between devices, swaps(): two = lax.ppermute(in_two, axis, pairs(1))  17.6 us
    ppermute x4, waiting for transfers between devices, swaps(): two = lax.ppermute(in_two, axis, pairs(1))  14.8 us
    pallas_call x1, Pallas kernels, root_of(): pl.pallas_call(root_kernel, out_shape=jax.ShapeDtypeStruct((members, memb...  6.38 us
    pallas_call x1, Pallas kernels, inner_forecast(): pl.pallas_call(inner_kernel, out_shape=(jax.ShapeDtypeStruct((patches, me...  4.26 us
  transfers between devices with their start and end apart: 8, of which 4 were waited for; matrix products, arithmetic and copies ran while one was open for 1% of the time, Pallas kernels for 4%

profile of v1, /device:TPU:56, one launch (start us, length us, event | category | flops | bytes accessed | tf_op | source)
XLA Modules:
  0.0 173.7 jit_solution(15151847014544128477)
XLA Ops:
  0.0 2.0 %ends.1 = (bf16[8,18432]{1,0:T(8,128)(2,1)S(1)}, bf16[8,18432]{1,0:T(8,128)(2,1)S(1)}, bf16[8,16,8192]{2,1,0:T(8,128)(2,1)S(1)}, f32[16,8192]{1,0:T(8,128)S(1)}) custom-call(bf16[8,16,8192]{2,1,0:T(8,128)(2,1)} %x_hbm.1, f32[16,8192]{1,0:T(8,128)} %field_hbm.1), custom_call_target="tpu_custom_call" | custom-call | tf_op jit(solution)/shard_map/ends/pallas_call | solution.py:110
  2.0 0.8 collective-permute-start
  2.8 5.4 %collective-permute-start.1 = (bf16[8,18432]{1,0:T(8,128)(2,1)S(1)}, bf16[8,18432]{1,0:T(8,128)(2,1)S(1)}, u32[]{:S(2)}, u32[]{:S(2)}) collective-permute-start(bf16[8,18432]{1,0:T(8,128)(2,1)S(1)} %get-tuple-element.19), channel_id=1, source_target_pairs={{1,2},{3,4},{5,6},{2,1},{4,3},{6,5},{9,10},{11,12},{13,14},{10,9},... | collective-permute-start | bytes 884744 | tf_op jit(solution)/shard_map/ppermute | solution.py:593
  8.3 1.2 copy.9
  9.4 4.3 %inner.1 = (bf16[32,8,4096]{2,1,0:T(8,128)(2,1)S(1)}, f32[4,8,8192]{2,1,0:T(8,128)S(1)}) custom-call(bf16[16,8,8192]{2,1,0:T(8,128)(2,1)S(1)} %bitcast.6, f32[16,8192]{1,0:T(8,128)S(1)} %get-tuple-element.20.field_ref.coef_ref), custom_call_target="tpu_custom_call" | custom-call | tf_op jit(solution)/shard_map/inner/pallas_call | solution.py:190
  13.7 3.1 %collective-permute-done.1.two_ref = bf16[8,18432]{1,0:T(8,128)(2,1)S(1)} collective-permute-done((bf16[8,18432]{1,0:T(8,128)(2,1)S(1)}, bf16[8,18432]{1,0:T(8,128)(2,1)S(1)}, u32[]{:S(2)}, u32[]{:S(2)}) %collective-permute-start.1) | collective-permute-done | bytes 294944 | tf_op jit(solution)/shard_map/ppermute | solution.py:593
  16.8 1.7 %outer.1 = bf16[32,8,4096]{2,1,0:T(8,128)(2,1)S(1)} custom-call(bf16[16,8,8192]{2,1,0:T(8,128)(2,1)S(1)} %bitcast.7, bf16[8,18432]{1,0:T(8,128)(2,1)S(1)} %collective-permute-done.one_ref, bf16[8,18432]{1,0:T(8,128)(2,1)S(1)} %collective-permute-done.1.two_ref, f32[16,8192]{1,0:T(8,128)S(1)} %get-tuple-element.20.field_ref.coef_ref, ...), custom_call_target="tpu_custom_call", output_to_operand_aliasing={{}: (4, {})} | custom-call | tf_op jit(solution)/shard_map/outer/pallas_call | solution.py:252
  18.6 61.0 %all_to_all.10.block_ref = bf16[32,8,4096]{2,1,0:T(8,128)(2,1)S(1)} all-to-all(bf16[32,8,4096]{2,1,0:T(8,128)(2,1)S(1)} %outer.1), channel_id=1, replica_groups=mesh['mem_0'=2,'mem_1'=8,'mem_2'=2,'space'=8] {'mem_0','mem_1','mem_2'}, dimensions={0} | all-to-all | bytes 4194304 | tf_op jit(solution)/shard_map/all_to_all | solution.py:612
  79.6 1.6 gram.1
  81.2 1.9 %collective-permute-start.3 = (f32[136,256]{1,0:T(8,128)S(1)}, f32[136,256]{1,0:T(8,128)S(1)}, u32[]{:S(2)}, u32[]{:S(2)}) collective-permute-start(f32[136,256]{1,0:T(8,128)S(1)} %gram.1), channel_id=1, source_target_pairs={{8,16},{24,32},{40,48},{56,64},{72,80},{88,96},{104,112},{120,128}... | collective-permute-start | bytes 417800 | tf_op jit(solution)/shard_map/ppermute | solution.py:593
  83.2 0.1 collective-permute-start.2
  83.3 4.3 %collective-permute-done.3 = f32[136,256]{1,0:T(8,128)S(1)} collective-permute-done((f32[136,256]{1,0:T(8,128)S(1)}, f32[136,256]{1,0:T(8,128)S(1)}, u32[]{:S(2)}, u32[]{:S(2)}) %collective-permute-start.3) | collective-permute-done | bytes 139296 | tf_op jit(solution)/shard_map/ppermute | solution.py:593
  87.6 5.1 %collective-permute-start.5 = (f32[136,256]{1,0:T(8,128)S(1)}, f32[136,256]{1,0:T(8,128)S(1)}, u32[]{:S(2)}, u32[]{:S(2)}) collective-permute-start(f32[136,256]{1,0:T(8,128)S(1)} %multiply_add_fusion.mid_ref), channel_id=1, source_target_pairs={{1,2},{3,4},{5,6},{2,1},{4,3},{6,5},{9,10},{11,12},{13,14},{10,9},... | collective-permute-start | bytes 417800 | tf_op jit(solution)/shard_map/ppermute | solution.py:593
  92.8 0.1 collective-permute-start.4
  92.9 0.8 center.1
  93.6 4.5 %collective-permute-done.5.two_ref = f32[136,256]{1,0:T(8,128)S(1)} collective-permute-done((f32[136,256]{1,0:T(8,128)S(1)}, f32[136,256]{1,0:T(8,128)S(1)}, u32[]{:S(2)}, u32[]{:S(2)}) %collective-permute-start.5) | collective-permute-done | bytes 139296 | tf_op jit(solution)/shard_map/ppermute | solution.py:593
  98.2 6.4 %root.1.turned_ref = bf16[256,256]{1,0:T(8,128)(2,1)S(1)} custom-call(f32[136,256]{1,0:T(8,128)S(1)} %collective-permute-done.4.one_ref, f32[136,256]{1,0:T(8,128)S(1)} %multiply_add_fusion.mid_ref, f32[136,256]{1,0:T(8,128)S(1)} %collective-permute-done.5.two_ref), custom_call_target="tpu_custom_call" | custom-call | tf_op jit(solution)/shard_map/root/pallas_call | solution.py:381
  104.6 1.2 update.1
  105.8 55.8 %all_to_all.11.block_ref = bf16[32,8,4096]{2,1,0:T(8,128)(2,1)S(1)} all-to-all(bf16[32,8,4096]{2,1,0:T(8,128)(2,1)S(1)} %update.1), channel_id=1, replica_groups=mesh['mem_0'=2,'mem_1'=8,'mem_2'=2,'space'=8] {'mem_0','mem_1','mem_2'}, dimensions={0} | all-to-all | bytes 4194304 | tf_op jit(solution)/shard_map/all_to_all | solution.py:621
  161.7 0.1 collective-permute-start.6
  161.8 5.1 %collective-permute-start.7 = (bf16[32,8,256]{2,1,0:T(8,128)(2,1)S(1)}, bf16[32,8,256]{2,1,0:T(8,128)(2,1)S(1)}, u32[]{:S(2)}, u32[]{:S(2)}) collective-permute-start(bf16[32,8,256]{2,1,0:T(8,128)(2,1)S(1)} %get-tuple-element.26), channel_id=1, source_target_pairs={{1,2},{3,4},{5,6},{2,1},{4,3},{6,5},{9,10},{11,12},{13,14},{10,9},... | collective-permute-start | bytes 393224 | tf_op jit(solution)/shard_map/ppermute | solution.py:593
  166.9 2.6 %middle.1 = (bf16[8,16,8192]{2,1,0:T(8,128)(2,1)S(1)}, f32[2,8,8192]{2,1,0:T(8,128)S(1)}) custom-call(bf16[32,8,4096]{2,1,0:T(8,128)(2,1)S(1)} %all_to_all.11.block_ref, f32[16,8192]{1,0:T(8,128)S(1)} %get-tuple-element.20.field_ref.coef_ref), custom_call_target="tpu_custom_call" | custom-call | tf_op jit(solution)/shard_map/middle/pallas_call | solution.py:519
  169.5 2.8 %collective-permute-done.7.two_ref = bf16[32,8,256]{2,1,0:T(8,128)(2,1)S(1)} collective-permute-done((bf16[32,8,256]{2,1,0:T(8,128)(2,1)S(1)}, bf16[32,8,256]{2,1,0:T(8,128)(2,1)S(1)}, u32[]{:S(2)}, u32[]{:S(2)}) %collective-permute-start.7) | collective-permute-done | bytes 131104 | tf_op jit(solution)/shard_map/ppermute | solution.py:593
  172.3 1.5 rim.1
  (12 shorter events, 0.1 us)
Async XLA Ops:
  2.0 11.7 %collective-permute-start = (bf16[8,18432]{1,0:T(8,128)(2,1)S(1)}, bf16[8,18432]{1,0:T(8,128)(2,1)S(1)}, u32[]{:S(2)}, u32[]{:S(2)}) collective-permute-start(bf16[8,18432]{1,0:T(8,128)(2,1)S(1)} %get-tuple-element.18), channel_id=1, source_target_pairs={{0,1},{2,3},{4,5},{6,7},{1,0},{3,2},{5,4},{7,6},{8,9},{10,11},{12,... | collective-permute-start | bytes 884744 | tf_op jit(solution)/shard_map/ppermute | solution.py:594
  2.8 14.0 %collective-permute-start.1 = (bf16[8,18432]{1,0:T(8,128)(2,1)S(1)}, bf16[8,18432]{1,0:T(8,128)(2,1)S(1)}, u32[]{:S(2)}, u32[]{:S(2)}) collective-permute-start(bf16[8,18432]{1,0:T(8,128)(2,1)S(1)} %get-tuple-element.19), channel_id=1, source_target_pairs={{1,2},{3,4},{5,6},{2,1},{4,3},{6,5},{9,10},{11,12},{13,14},{10,9},... | collective-permute-start | bytes 884744 | tf_op jit(solution)/shard_map/ppermute | solution.py:593
  18.6 61.1 %copy-start = (s32[1,1,512]{2,1,0:T(1,128)S(1)}, s32[1,1,512]{2,1,0:T(1,128)}, u32[]{:S(2)}) copy-start(s32[1,1,512]{2,1,0:T(1,128)} %param.7) | copy-start | bytes 6148
  18.6 61.1 %copy-start.1 = (f32[1,1,512]{2,1,0:T(1,128)S(1)}, f32[1,1,512]{2,1,0:T(1,128)}, u32[]{:S(2)}) copy-start(f32[1,1,512]{2,1,0:T(1,128)} %param.8) | copy-start | bytes 6148
  18.6 61.0 %copy-start.2 = (f32[1,1,512]{2,1,0:T(1,128)S(1)}, f32[1,1,512]{2,1,0:T(1,128)}, u32[]{:S(2)}) copy-start(f32[1,1,512]{2,1,0:T(1,128)} %param.9) | copy-start | bytes 6148
  81.2 6.4 %collective-permute-start.3 = (f32[136,256]{1,0:T(8,128)S(1)}, f32[136,256]{1,0:T(8,128)S(1)}, u32[]{:S(2)}, u32[]{:S(2)}) collective-permute-start(f32[136,256]{1,0:T(8,128)S(1)} %gram.1), channel_id=1, source_target_pairs={{8,16},{24,32},{40,48},{56,64},{72,80},{88,96},{104,112},{120,128}... | collective-permute-start | bytes 417800 | tf_op jit(solution)/shard_map/ppermute | solution.py:593
  83.2 4.4 %collective-permute-start.2 = (f32[136,256]{1,0:T(8,128)S(1)}, f32[136,256]{1,0:T(8,128)S(1)}, u32[]{:S(2)}, u32[]{:S(2)}) collective-permute-start(f32[136,256]{1,0:T(8,128)S(1)} %gram.1), channel_id=1, source_target_pairs={{0,8},{16,24},{32,40},{48,56},{64,72},{80,88},{96,104},{112,120},{... | collective-permute-start | bytes 417800 | tf_op jit(solution)/shard_map/ppermute | solution.py:594
  87.6 10.6 %collective-permute-start.5 = (f32[136,256]{1,0:T(8,128)S(1)}, f32[136,256]{1,0:T(8,128)S(1)}, u32[]{:S(2)}, u32[]{:S(2)}) collective-permute-start(f32[136,256]{1,0:T(8,128)S(1)} %multiply_add_fusion.mid_ref), channel_id=1, source_target_pairs={{1,2},{3,4},{5,6},{2,1},{4,3},{6,5},{9,10},{11,12},{13,14},{10,9},... | collective-permute-start | bytes 417800 | tf_op jit(solution)/shard_map/ppermute | solution.py:593
  92.8 5.4 %collective-permute-start.4 = (f32[136,256]{1,0:T(8,128)S(1)}, f32[136,256]{1,0:T(8,128)S(1)}, u32[]{:S(2)}, u32[]{:S(2)}) collective-permute-start(f32[136,256]{1,0:T(8,128)S(1)} %multiply_add_fusion.mid_ref), channel_id=1, source_target_pairs={{0,1},{2,3},{4,5},{6,7},{1,0},{3,2},{5,4},{7,6},{8,9},{10,11},{12,... | collective-permute-start | bytes 417800 | tf_op jit(solution)/shard_map/ppermute | solution.py:594
  161.7 7.8 %collective-permute-start.6 = (bf16[32,8,256]{2,1,0:T(8,128)(2,1)S(1)}, bf16[32,8,256]{2,1,0:T(8,128)(2,1)S(1)}, u32[]{:S(2)}, u32[]{:S(2)}) collective-permute-start(bf16[32,8,256]{2,1,0:T(8,128)(2,1)S(1)} %get-tuple-element.25), channel_id=1, source_target_pairs={{0,1},{2,3},{4,5},{6,7},{1,0},{3,2},{5,4},{7,6},{8,9},{10,11},{12,... | collective-permute-start | bytes 393224 | tf_op jit(solution)/shard_map/ppermute | solution.py:594
  161.8 10.5 %collective-permute-start.7 = (bf16[32,8,256]{2,1,0:T(8,128)(2,1)S(1)}, bf16[32,8,256]{2,1,0:T(8,128)(2,1)S(1)}, u32[]{:S(2)}, u32[]{:S(2)}) collective-permute-start(bf16[32,8,256]{2,1,0:T(8,128)(2,1)S(1)} %get-tuple-element.26), channel_id=1, source_target_pairs={{1,2},{3,4},{5,6},{2,1},{4,3},{6,5},{9,10},{11,12},{13,14},{10,9},... | collective-permute-start | bytes 393224 | tf_op jit(solution)/shard_map/ppermute | solution.py:593
